TPU v7x, 32 devices: a whole 2x2x4 slice. The times are simulated.
32 devices in a mesh: blk: 8 (over z, x), grp: 4 (over y, core).
Axes of the slice: x: 2, y: 2, z: 4, core: 2. Of those that a mesh axis runs over, the one named last changes fastest.
Arguments:
- source_coords: float32 [3, 20480], P(None, ('blk', 'grp')), may hold values from 0 to 8, as said below
- source_values: float32 [3, 20480], P(None, ('blk', 'grp')), may hold values from -48 to 48
- target_coords: float32 [3, 16384], P(None, ('blk', 'grp')), may hold values from 0 to 8, as said below
- target_owner: int32 [16384], P(('blk', 'grp')), may hold values from 0 to 7, as said below
Outputs:
- weights: float32 [3, 20480], P(None, ('blk', 'grp'))
- poly: float32 [3, 4], replicated
- mapped: float32 [3, 16384], P(None, ('blk', 'grp'))
Inputs may be any that keep to these rules, and one draw needn't show every extreme that they name: `source_coords`: source vertex j has its first coordinate between j // 2560 and j // 2560 + 1, and the other two between 0 and 1. `target_coords`: target vertex t has its first coordinate between target_owner[t] and target_owner[t] + 1, and the other two between 0 and 1. target_owner[t] differs from t // 2048 by at most one.
All inputs are finite; a program needn't handle non-finite values.
Results may differ from a plain program's by a relative error of at most 0.0003.
Values sent between devices are 32-bit elements; how exact they have to be, the bound alone decides.
A program may use at most 64 MiB of HBM per device.

v0:
```python
import math
import jax
import jax.numpy as jnp
from jax import lax
from jax.sharding import PartitionSpec as P

ITERS = 3
REACH = 2
precise = lax.Precision.HIGHEST
thin_factor = 0.6
tiny = 1e-06


def from_behind(value, axis, steps):
    count = lax.axis_size(axis)
    initial, last = (max(0, -steps), min(count, count - steps))
    return lax.ppermute(value, axis, [(source, source + steps) for source in range(initial, last)])


def kernel_tile(rows, cols, stretch):
    along = rows[0][None, :] - cols[0][:, None]
    across = rows[1][None, :] - cols[1][:, None]
    upward = rows[2][None, :] - cols[2][:, None]
    return jnp.exp(-(thin_factor * along * along + stretch * (across * across + upward * upward)))


def basis(points, partitions, sources):
    ones = jnp.ones_like(points[0])
    stacked = jnp.stack(
        [ones, 2.0 * points[0] / partitions - 1.0, 2.0 * points[1] - 1.0, 2.0 * points[2] - 1.0]
    )
    return stacked / math.sqrt(sources)


def least_squares(hessenberg, beta):
    count = len(hessenberg)
    right_side = [beta] + [jnp.zeros_like(beta) for k in range(count)]
    upper = []
    cosines = []
    sines = []
    for k in range(count):
        column = list(hessenberg[k])
        for i in range(k):
            top = cosines[i] * column[i] + sines[i] * column[i + 1]
            lower = -sines[i] * column[i] + cosines[i] * column[i + 1]
            column[i] = top
            column[i + 1] = lower
        radius = jnp.sqrt(column[k] * column[k] + column[k + 1] * column[k + 1])
        cosine = column[k] / radius
        sine = column[k + 1] / radius
        column[k] = radius
        cosines.append(cosine)
        sines.append(sine)
        right_side[k + 1] = -sine * right_side[k]
        right_side[k] = cosine * right_side[k]
        upper.append(column[: k + 1])
    solved = [None] * count
    for k in reversed(range(count)):
        running = right_side[k]
        for j in range(k + 1, count):
            running = running - upper[j][k] * solved[j]
        solved[k] = running / upper[k][k]
    return solved


def near_slabs(block, reach):
    slab = lax.all_gather(block, "grp", axis=1, tiled=True)
    pieces = []
    for offset in range(-reach, reach + 1):
        if offset == 0:
            pieces.append(slab)
        else:
            pieces.append(from_behind(slab, "blk", -offset))
    return jnp.stack(pieces)


def apply_near(rows, near_coords, near_values, owners, first_slab, stretch, reach):
    labels = jnp.arange(near_coords.shape[0], dtype=jnp.int32) + first_slab

    def add_slab(running, item):
        cols, values, slab = item
        tile = kernel_tile(rows, cols, stretch)
        if owners is not None:
            tile = jnp.where((jnp.abs(owners - slab) <= reach)[None, :], tile, 0.0)
        return (
            running + jnp.dot(values, tile, precision=precise, preferred_element_type=jnp.float32),
            None,
        )

    start = jnp.zeros((near_values.shape[1], rows.shape[1]), jnp.float32)
    result, unused = lax.scan(add_slab, start, (near_coords, near_values, labels))
    return result


def shards(source_coords, source_values, target_coords, target_owner):
    reach = REACH
    own_rows = source_coords.shape[1]
    slab_len = own_rows * lax.axis_size("grp")
    partitions = lax.axis_size("blk")
    sources = slab_len * partitions
    stretch = 4.0 * slab_len
    here = lax.axis_index("blk")
    poly_src = basis(source_coords, partitions, sources)
    start_sq, start_moment = lax.psum(
        (
            jnp.sum(source_values * source_values, axis=1),
            jnp.dot(
                source_values, poly_src.T, precision=precise, preferred_element_type=jnp.float32
            ),
        ),
        ("blk", "grp"),
    )
    beta = jnp.sqrt(start_sq + tiny)
    heads = [source_values / beta[:, None]]
    tails = [jnp.zeros_like(start_moment)]
    moments = [start_moment / beta[:, None]]
    hessenberg = []
    for k in range(ITERS):
        both_near = near_slabs(jnp.concatenate([source_coords, heads[k]], axis=0), reach)
        cols = both_near[:, :3]
        values_near = both_near[:, 3:]
        image_head = apply_near(
            source_coords, cols, values_near, None, here - reach, stretch, reach
        ) + jnp.dot(tails[k], poly_src, precision=precise, preferred_element_type=jnp.float32)
        image_tail = moments[k]
        column = []
        local_dots = jnp.stack(
            [jnp.sum(heads[i] * image_head, axis=1) for i in range(k + 1)], axis=1
        )
        head_dots, image_sq, image_moment = lax.psum(
            (
                local_dots,
                jnp.sum(image_head * image_head, axis=1),
                jnp.dot(
                    image_head, poly_src.T, precision=precise, preferred_element_type=jnp.float32
                ),
            ),
            ("blk", "grp"),
        )
        full_sq = image_sq + jnp.sum(image_tail * image_tail, axis=1)
        rest_head = image_head
        rest_tail = image_tail
        rest_moment = image_moment
        for i in range(k + 1):
            factor = head_dots[:, i] + jnp.sum(tails[i] * image_tail, axis=1)
            full_sq = full_sq - factor * factor
            rest_head = rest_head - factor[:, None] * heads[i]
            rest_tail = rest_tail - factor[:, None] * tails[i]
            rest_moment = rest_moment - factor[:, None] * moments[i]
            column.append(factor)
        length = jnp.sqrt(full_sq + tiny)
        column.append(length)
        hessenberg.append(column)
        heads.append(rest_head / length[:, None])
        tails.append(rest_tail / length[:, None])
        moments.append(rest_moment / length[:, None])
    solved = least_squares(hessenberg, beta)
    weights = solved[0][:, None] * heads[0]
    poly = solved[0][:, None] * tails[0]
    for k in range(1, ITERS):
        weights = weights + solved[k][:, None] * heads[k]
        poly = poly + solved[k][:, None] * tails[k]
    joined_near = near_slabs(jnp.concatenate([source_coords, weights], axis=0), reach + 1)
    cols_far = joined_near[:, :3]
    weights_near = joined_near[:, 3:]
    poly_tgt = basis(target_coords, partitions, sources)
    mapped = apply_near(
        target_coords, cols_far, weights_near, target_owner, here - reach - 1, stretch, reach
    )
    mapped = mapped + jnp.dot(poly, poly_tgt, precision=precise, preferred_element_type=jnp.float32)
    return (weights, poly, mapped)


def solution(mesh):
    return jax.shard_map(
        shards,
        mesh=mesh,
        in_specs=(
            P(None, ("blk", "grp")),
            P(None, ("blk", "grp")),
            P(None, ("blk", "grp")),
            P(("blk", "grp")),
        ),
        out_specs=(P(None, ("blk", "grp")), P(), P(None, ("blk", "grp"))),
        check_vma=False,
    )
```

profile of v0, /device:TPU:6, one launch (start us, length us, event | category | flops | bytes accessed | tf_op | source)
XLA Modules:
  0.0 393.1 jit_solution(17570499681100357009)
XLA Ops:
  1.5 40.3 %psum.70 = f32[3]{0:T(128)S(1)} all-reduce(f32[3]{0:T(128)S(1)} %multiply_reduce_fusion.9), channel_id=1, replica_groups=mesh['blk'=8,'grp'=4] {'blk','grp'}, use_global_device_ids=true, to_apply=%region_1.0 | all-reduce | flops 3 | bytes 24 | tf_op jit(solution)/shard_map/psum | solution.py:104
  43.3 5.3 %all_gather.12 = f32[6,2560]{1,0:T(8,128)S(1)} all-gather(f32[6,640]{1,0:T(8,128)S(1)} %pad_maximum_fusion.3), channel_id=1, replica_groups=mesh['blk'=8,'grp'=4] {'grp'}, dimensions={1}, use_global_device_ids=true | all-gather | bytes 76800 | tf_op jit(solution)/shard_map/all_gather | solution.py:67
  48.5 3.4 collective-permute-start
  52.0 4.2 %collective-permute-start.1 = (f32[6,2560]{1,0:T(8,128)S(1)}, f32[6,2560]{1,0:T(8,128)S(1)}, u32[]{:S(2)}, u32[]{:S(2)}) collective-permute-start(f32[6,2560]{1,0:T(8,128)S(1)} %all_gather.12), channel_id=1, source_target_pairs={{0,4},{4,8},{8,12},{12,16},{16,20},{20,24},{24,28},{1,5},{5,9},{9,... | collective-permute-start | bytes 184328 | tf_op jit(solution)/shard_map/ppermute | solution.py:17
  64.5 29.7 %while.44 = (s32[]{:T(128)}, f32[3,640]{1,0:T(4,128)S(1)}, f32[5,3,2560]{2,1,0:T(4,128)S(1)}, f32[3,640]{1,0:T(4,128)S(1)}, f32[5,3,2560]{2,1,0:T(4,128)S(1)}, /*index=5*/s32[]{:T(128)}, s32[]{:T(128)}, s32[]{}, s32[]{}) while((s32[]{:T(128)}, f32[3,640]{1,0:T(4,128)S(1)}, f32[5,3,2560]{2,1,0:T(4,128)S(1)}, ...), condition=%wide.region_3.4_spmd.clone, body=%wide.region_2.0_spmd.clone.sunk | while | flops 77008640 | bytes 184975 | solution.py:91
  64.7 5.8 %fusion.163 = f32[3,640]{1,0:T(4,128)S(1)} fusion(f32[2560]{0:T(1024)S(1)} %get-tuple-element.469, f32[640]{0:T(1024)S(1)} %get-tuple-element.470, f32[2560]{0:T(1024)S(1)} %get-tuple-element.471, f32[640]{0:T(1024)S(1)} %get-tuple-element.472, f32[2560]{0:T(1024)S(1)} %get-tuple-element.473, f32[640]{0:T(1024)S(1)} %get-tuple-element.474, ...), kind=kOutput, calls=%fused_computation.20.clone.1 | convolution fusion | flops 77008640 | bytes 108037 | tf_op jit(solution)/shard_map/while/body/eval_jaxpr/dot_general | solution.py:86
  70.6 5.8 %fusion.163 = f32[3,640]{1,0:T(4,128)S(1)} fusion(f32[2560]{0:T(1024)S(1)} %get-tuple-element.469, f32[640]{0:T(1024)S(1)} %get-tuple-element.470, f32[2560]{0:T(1024)S(1)} %get-tuple-element.471, f32[640]{0:T(1024)S(1)} %get-tuple-element.472, f32[2560]{0:T(1024)S(1)} %get-tuple-element.473, f32[640]{0:T(1024)S(1)} %get-tuple-element.474, ...), kind=kOutput, calls=%fused_computation.20.clone.1 | convolution fusion | flops 77008640 | bytes 108037 | tf_op jit(solution)/shard_map/while/body/eval_jaxpr/dot_general | solution.py:86
  76.6 5.8 %fusion.163 = f32[3,640]{1,0:T(4,128)S(1)} fusion(f32[2560]{0:T(1024)S(1)} %get-tuple-element.469, f32[640]{0:T(1024)S(1)} %get-tuple-element.470, f32[2560]{0:T(1024)S(1)} %get-tuple-element.471, f32[640]{0:T(1024)S(1)} %get-tuple-element.472, f32[2560]{0:T(1024)S(1)} %get-tuple-element.473, f32[640]{0:T(1024)S(1)} %get-tuple-element.474, ...), kind=kOutput, calls=%fused_computation.20.clone.1 | convolution fusion | flops 77008640 | bytes 108037 | tf_op jit(solution)/shard_map/while/body/eval_jaxpr/dot_general | solution.py:86
  82.5 5.8 %fusion.163 = f32[3,640]{1,0:T(4,128)S(1)} fusion(f32[2560]{0:T(1024)S(1)} %get-tuple-element.469, f32[640]{0:T(1024)S(1)} %get-tuple-element.470, f32[2560]{0:T(1024)S(1)} %get-tuple-element.471, f32[640]{0:T(1024)S(1)} %get-tuple-element.472, f32[2560]{0:T(1024)S(1)} %get-tuple-element.473, f32[640]{0:T(1024)S(1)} %get-tuple-element.474, ...), kind=kOutput, calls=%fused_computation.20.clone.1 | convolution fusion | flops 77008640 | bytes 108037 | tf_op jit(solution)/shard_map/while/body/eval_jaxpr/dot_general | solution.py:86
  88.4 5.8 %fusion.163 = f32[3,640]{1,0:T(4,128)S(1)} fusion(f32[2560]{0:T(1024)S(1)} %get-tuple-element.469, f32[640]{0:T(1024)S(1)} %get-tuple-element.470, f32[2560]{0:T(1024)S(1)} %get-tuple-element.471, f32[640]{0:T(1024)S(1)} %get-tuple-element.472, f32[2560]{0:T(1024)S(1)} %get-tuple-element.473, f32[640]{0:T(1024)S(1)} %get-tuple-element.474, ...), kind=kOutput, calls=%fused_computation.20.clone.1 | convolution fusion | flops 77008640 | bytes 108037 | tf_op jit(solution)/shard_map/while/body/eval_jaxpr/dot_general | solution.py:86
  94.6 41.4 %all-reduce.2 = (f32[3]{0:T(128)S(1)}, f32[3,4]{1,0:T(4,128)S(1)}, f32[3,1]{0,1:T(1,128)S(1)}) all-reduce(f32[3]{0:T(128)S(1)} %get-tuple-element.232, f32[3,4]{1,0:T(4,128)S(1)} %convolution_bitcast_fusion, f32[3,1]{0,1:T(1,128)S(1)} %bitcast.208), channel_id=1, replica_groups=mesh['blk'=8,'grp'=4] {'blk','grp'}, use_global_device_ids=true, to_apply=%region_9.10 | all-reduce | flops 18 | bytes 144 | tf_op jit(solution)/shard_map/psum | solution.py:130
  136.3 5.3 %all_gather.13 = f32[6,2560]{1,0:T(8,128)S(1)} all-gather(f32[6,640]{1,0:T(8,128)S(1)} %pad_maximum_fusion.2), channel_id=1, replica_groups=mesh['blk'=8,'grp'=4] {'grp'}, dimensions={1}, use_global_device_ids=true | all-gather | bytes 76800 | tf_op jit(solution)/shard_map/all_gather | solution.py:67
  143.5 2.8 collective-permute-start.5
  146.4 3.0 collective-permute-start.6
  151.2 2.6 collective-permute-done.6
  155.8 29.7 %while.45 = (s32[]{:T(128)}, f32[3,640]{1,0:T(4,128)S(1)}, f32[5,3,2560]{2,1,0:T(4,128)S(1)}, f32[3,640]{1,0:T(4,128)S(1)}, f32[5,3,2560]{2,1,0:T(4,128)S(1)}, /*index=5*/s32[]{:T(128)}, s32[]{:T(128)}, s32[]{}, s32[]{}) while((s32[]{:T(128)}, f32[3,640]{1,0:T(4,128)S(1)}, f32[5,3,2560]{2,1,0:T(4,128)S(1)}, ...), condition=%wide.region_12.13_spmd.clone, body=%wide.region_11.12_spmd.clone.sunk | while | flops 77008640 | bytes 184975 | solution.py:91
  156.0 5.8 %fusion.166 = f32[3,640]{1,0:T(4,128)S(1)} fusion(f32[2560]{0:T(1024)S(1)} %get-tuple-element.480, f32[640]{0:T(1024)S(1)} %get-tuple-element.481, f32[2560]{0:T(1024)S(1)} %get-tuple-element.482, f32[640]{0:T(1024)S(1)} %get-tuple-element.483, f32[2560]{0:T(1024)S(1)} %get-tuple-element.484, f32[640]{0:T(1024)S(1)} %get-tuple-element.485, ...), kind=kOutput, calls=%fused_computation.52.clone.1 | convolution fusion | flops 77008640 | bytes 108037 | tf_op jit(solution)/shard_map/while/body/eval_jaxpr/dot_general | solution.py:86
  161.9 5.8 %fusion.166 = f32[3,640]{1,0:T(4,128)S(1)} fusion(f32[2560]{0:T(1024)S(1)} %get-tuple-element.480, f32[640]{0:T(1024)S(1)} %get-tuple-element.481, f32[2560]{0:T(1024)S(1)} %get-tuple-element.482, f32[640]{0:T(1024)S(1)} %get-tuple-element.483, f32[2560]{0:T(1024)S(1)} %get-tuple-element.484, f32[640]{0:T(1024)S(1)} %get-tuple-element.485, ...), kind=kOutput, calls=%fused_computation.52.clone.1 | convolution fusion | flops 77008640 | bytes 108037 | tf_op jit(solution)/shard_map/while/body/eval_jaxpr/dot_general | solution.py:86
  167.8 5.8 %fusion.166 = f32[3,640]{1,0:T(4,128)S(1)} fusion(f32[2560]{0:T(1024)S(1)} %get-tuple-element.480, f32[640]{0:T(1024)S(1)} %get-tuple-element.481, f32[2560]{0:T(1024)S(1)} %get-tuple-element.482, f32[640]{0:T(1024)S(1)} %get-tuple-element.483, f32[2560]{0:T(1024)S(1)} %get-tuple-element.484, f32[640]{0:T(1024)S(1)} %get-tuple-element.485, ...), kind=kOutput, calls=%fused_computation.52.clone.1 | convolution fusion | flops 77008640 | bytes 108037 | tf_op jit(solution)/shard_map/while/body/eval_jaxpr/dot_general | solution.py:86
  173.8 5.8 %fusion.166 = f32[3,640]{1,0:T(4,128)S(1)} fusion(f32[2560]{0:T(1024)S(1)} %get-tuple-element.480, f32[640]{0:T(1024)S(1)} %get-tuple-element.481, f32[2560]{0:T(1024)S(1)} %get-tuple-element.482, f32[640]{0:T(1024)S(1)} %get-tuple-element.483, f32[2560]{0:T(1024)S(1)} %get-tuple-element.484, f32[640]{0:T(1024)S(1)} %get-tuple-element.485, ...), kind=kOutput, calls=%fused_computation.52.clone.1 | convolution fusion | flops 77008640 | bytes 108037 | tf_op jit(solution)/shard_map/while/body/eval_jaxpr/dot_general | solution.py:86
  179.7 5.8 %fusion.166 = f32[3,640]{1,0:T(4,128)S(1)} fusion(f32[2560]{0:T(1024)S(1)} %get-tuple-element.480, f32[640]{0:T(1024)S(1)} %get-tuple-element.481, f32[2560]{0:T(1024)S(1)} %get-tuple-element.482, f32[640]{0:T(1024)S(1)} %get-tuple-element.483, f32[2560]{0:T(1024)S(1)} %get-tuple-element.484, f32[640]{0:T(1024)S(1)} %get-tuple-element.485, ...), kind=kOutput, calls=%fused_computation.52.clone.1 | convolution fusion | flops 77008640 | bytes 108037 | tf_op jit(solution)/shard_map/while/body/eval_jaxpr/dot_general | solution.py:86
  185.9 40.5 %all-reduce.1 = (f32[3]{0:T(128)S(1)}, f32[3,4]{1,0:T(4,128)S(1)}, f32[3,2]{0,1:T(2,128)S(1)}) all-reduce(f32[3]{0:T(128)S(1)} %get-tuple-element.229, f32[3,4]{1,0:T(4,128)S(1)} %fusion.135, f32[3,2]{0,1:T(2,128)S(1)} %pad_maximum_fusion.5), channel_id=1, replica_groups=mesh['blk'=8,'grp'=4] {'blk','grp'}, use_global_device_ids=true, to_apply=%region_20.21 | all-reduce | flops 21 | bytes 168 | tf_op jit(solution)/shard_map/psum | solution.py:130
  226.7 5.3 %all_gather.14 = f32[6,2560]{1,0:T(8,128)S(1)} all-gather(f32[6,640]{1,0:T(8,128)S(1)} %pad_maximum_fusion.1), channel_id=1, replica_groups=mesh['blk'=8,'grp'=4] {'grp'}, dimensions={1}, use_global_device_ids=true | all-gather | bytes 76800 | tf_op jit(solution)/shard_map/all_gather | solution.py:67
  232.0 2.1 collective-permute-start.8
  234.1 3.6 collective-permute-start.9
  237.7 2.2 collective-permute-start.10
  241.9 3.2 collective-permute-done.10
  246.4 29.7 %while.46 = (s32[]{:T(128)}, f32[3,640]{1,0:T(4,128)S(1)}, f32[5,3,2560]{2,1,0:T(4,128)S(1)}, f32[3,640]{1,0:T(4,128)S(1)}, f32[5,3,2560]{2,1,0:T(4,128)S(1)}, /*index=5*/s32[]{:T(128)}, s32[]{:T(128)}, s32[]{}, s32[]{}) while((s32[]{:T(128)}, f32[3,640]{1,0:T(4,128)S(1)}, f32[5,3,2560]{2,1,0:T(4,128)S(1)}, ...), condition=%wide.region_23.24_spmd.clone, body=%wide.region_22.23_spmd.clone.sunk | while | flops 77008640 | bytes 184975 | solution.py:91
  246.5 5.8 %fusion.169 = f32[3,640]{1,0:T(4,128)S(1)} fusion(f32[2560]{0:T(1024)S(1)} %get-tuple-element.491, f32[640]{0:T(1024)S(1)} %get-tuple-element.492, f32[2560]{0:T(1024)S(1)} %get-tuple-element.493, f32[640]{0:T(1024)S(1)} %get-tuple-element.494, f32[2560]{0:T(1024)S(1)} %get-tuple-element.495, f32[640]{0:T(1024)S(1)} %get-tuple-element.496, ...), kind=kOutput, calls=%fused_computation.84.clone.1 | convolution fusion | flops 77008640 | bytes 108037 | tf_op jit(solution)/shard_map/while/body/eval_jaxpr/dot_general | solution.py:86
  252.5 5.8 %fusion.169 = f32[3,640]{1,0:T(4,128)S(1)} fusion(f32[2560]{0:T(1024)S(1)} %get-tuple-element.491, f32[640]{0:T(1024)S(1)} %get-tuple-element.492, f32[2560]{0:T(1024)S(1)} %get-tuple-element.493, f32[640]{0:T(1024)S(1)} %get-tuple-element.494, f32[2560]{0:T(1024)S(1)} %get-tuple-element.495, f32[640]{0:T(1024)S(1)} %get-tuple-element.496, ...), kind=kOutput, calls=%fused_computation.84.clone.1 | convolution fusion | flops 77008640 | bytes 108037 | tf_op jit(solution)/shard_map/while/body/eval_jaxpr/dot_general | solution.py:86
  258.4 5.8 %fusion.169 = f32[3,640]{1,0:T(4,128)S(1)} fusion(f32[2560]{0:T(1024)S(1)} %get-tuple-element.491, f32[640]{0:T(1024)S(1)} %get-tuple-element.492, f32[2560]{0:T(1024)S(1)} %get-tuple-element.493, f32[640]{0:T(1024)S(1)} %get-tuple-element.494, f32[2560]{0:T(1024)S(1)} %get-tuple-element.495, f32[640]{0:T(1024)S(1)} %get-tuple-element.496, ...), kind=kOutput, calls=%fused_computation.84.clone.1 | convolution fusion | flops 77008640 | bytes 108037 | tf_op jit(solution)/shard_map/while/body/eval_jaxpr/dot_general | solution.py:86
  264.3 5.8 %fusion.169 = f32[3,640]{1,0:T(4,128)S(1)} fusion(f32[2560]{0:T(1024)S(1)} %get-tuple-element.491, f32[640]{0:T(1024)S(1)} %get-tuple-element.492, f32[2560]{0:T(1024)S(1)} %get-tuple-element.493, f32[640]{0:T(1024)S(1)} %get-tuple-element.494, f32[2560]{0:T(1024)S(1)} %get-tuple-element.495, f32[640]{0:T(1024)S(1)} %get-tuple-element.496, ...), kind=kOutput, calls=%fused_computation.84.clone.1 | convolution fusion | flops 77008640 | bytes 108037 | tf_op jit(solution)/shard_map/while/body/eval_jaxpr/dot_general | solution.py:86
  270.3 5.8 %fusion.169 = f32[3,640]{1,0:T(4,128)S(1)} fusion(f32[2560]{0:T(1024)S(1)} %get-tuple-element.491, f32[640]{0:T(1024)S(1)} %get-tuple-element.492, f32[2560]{0:T(1024)S(1)} %get-tuple-element.493, f32[640]{0:T(1024)S(1)} %get-tuple-element.494, f32[2560]{0:T(1024)S(1)} %get-tuple-element.495, f32[640]{0:T(1024)S(1)} %get-tuple-element.496, ...), kind=kOutput, calls=%fused_computation.84.clone.1 | convolution fusion | flops 77008640 | bytes 108037 | tf_op jit(solution)/shard_map/while/body/eval_jaxpr/dot_general | solution.py:86
  276.5 41.9 %all-reduce = (f32[3]{0:T(128)S(1)}, f32[3,4]{1,0:T(4,128)S(1)}, f32[3,3]{0,1:T(4,128)S(1)}) all-reduce(f32[3]{0:T(128)S(1)} %get-tuple-element.225, f32[3,4]{1,0:T(4,128)S(1)} %fusion.134, f32[3,3]{0,1:T(4,128)S(1)} %pad_maximum_fusion.4), channel_id=1, replica_groups=mesh['blk'=8,'grp'=4] {'blk','grp'}, use_global_device_ids=true, to_apply=%region_33.34 | all-reduce | flops 24 | bytes 192 | tf_op jit(solution)/shard_map/psum | solution.py:130
  318.8 5.3 %all_gather.15 = f32[6,2560]{1,0:T(8,128)S(1)} all-gather(f32[6,640]{1,0:T(8,128)S(1)} %pad_maximum_fusion), channel_id=1, replica_groups=mesh['blk'=8,'grp'=4] {'grp'}, dimensions={1}, use_global_device_ids=true | all-gather | bytes 76800 | tf_op jit(solution)/shard_map/all_gather | solution.py:67
  324.1 2.2 collective-permute-start.12
  326.3 4.0 %collective-permute-start.13 = (f32[6,2560]{1,0:T(8,128)S(1)}, f32[6,2560]{1,0:T(8,128)S(1)}, u32[]{:S(2)}, u32[]{:S(2)}) collective-permute-start(f32[6,2560]{1,0:T(8,128)S(1)} %all_gather.15), channel_id=1, source_target_pairs={{0,8},{4,12},{8,16},{12,20},{16,24},{20,28},{1,9},{5,13},{9,17},{1... | collective-permute-start | bytes 184328 | tf_op jit(solution)/shard_map/ppermute | solution.py:17
  330.3 3.8 collective-permute-start.14
  339.2 2.6 collective-permute-done.15
  342.9 5.3 %collective-permute-done.17 = f32[6,2560]{1,0:T(8,128)S(1)} collective-permute-done((f32[6,2560]{1,0:T(8,128)S(1)}, f32[6,2560]{1,0:T(8,128)S(1)}, u32[]{:S(2)}, u32[]{:S(2)}) %collective-permute-start.17) | collective-permute-done | bytes 61472 | tf_op jit(solution)/shard_map/ppermute | solution.py:17
  348.9 43.3 %while.47 = (s32[]{:T(128)}, f32[3,512]{1,0:T(4,128)S(1)}, f32[7,3,2560]{2,1,0:T(4,128)S(1)}, s32[7]{0:T(128)S(1)}, s32[512]{0:T(512)S(1)}, /*index=5*/f32[3,512...) while((s32[]{:T(128)}, f32[3,512]{1,0:T(4,128)S(1)}, ...), condition=%wide.region_36.37_spmd.clone, body=%wide.region_35.36_spmd.clone.sunk | while | flops 62919172 | bytes 175279 | solution.py:91
  350.3 4.8 %fusion.173 = f32[3,512]{1,0:T(4,128)S(1)} fusion(f32[2560]{0:T(1024)S(1)} %get-tuple-element.504, f32[512]{0:T(512)S(1)} %bitcast.203, f32[2560]{0:T(1024)S(1)} %get-tuple-element.506, f32[512]{0:T(512)S(1)} %bitcast.204, f32[2560]{0:T(1024)S(1)} %get-tuple-element.508, f32[512]{0:T(512)S(1)} %bitcast.202, ...), kind=kOutput, calls=%fused_computation.119.clone.1 | convolution fusion | flops 62917632 | bytes 98821 | tf_op jit(solution)/shard_map/while/body/eval_jaxpr/dot_general | solution.py:86
  356.5 4.8 %fusion.173 = f32[3,512]{1,0:T(4,128)S(1)} fusion(f32[2560]{0:T(1024)S(1)} %get-tuple-element.504, f32[512]{0:T(512)S(1)} %bitcast.203, f32[2560]{0:T(1024)S(1)} %get-tuple-element.506, f32[512]{0:T(512)S(1)} %bitcast.204, f32[2560]{0:T(1024)S(1)} %get-tuple-element.508, f32[512]{0:T(512)S(1)} %bitcast.202, ...), kind=kOutput, calls=%fused_computation.119.clone.1 | convolution fusion | flops 62917632 | bytes 98821 | tf_op jit(solution)/shard_map/while/body/eval_jaxpr/dot_general | solution.py:86
  362.7 4.8 %fusion.173 = f32[3,512]{1,0:T(4,128)S(1)} fusion(f32[2560]{0:T(1024)S(1)} %get-tuple-element.504, f32[512]{0:T(512)S(1)} %bitcast.203, f32[2560]{0:T(1024)S(1)} %get-tuple-element.506, f32[512]{0:T(512)S(1)} %bitcast.204, f32[2560]{0:T(1024)S(1)} %get-tuple-element.508, f32[512]{0:T(512)S(1)} %bitcast.202, ...), kind=kOutput, calls=%fused_computation.119.clone.1 | convolution fusion | flops 62917632 | bytes 98821 | tf_op jit(solution)/shard_map/while/body/eval_jaxpr/dot_general | solution.py:86
  368.9 4.8 %fusion.173 = f32[3,512]{1,0:T(4,128)S(1)} fusion(f32[2560]{0:T(1024)S(1)} %get-tuple-element.504, f32[512]{0:T(512)S(1)} %bitcast.203, f32[2560]{0:T(1024)S(1)} %get-tuple-element.506, f32[512]{0:T(512)S(1)} %bitcast.204, f32[2560]{0:T(1024)S(1)} %get-tuple-element.508, f32[512]{0:T(512)S(1)} %bitcast.202, ...), kind=kOutput, calls=%fused_computation.119.clone.1 | convolution fusion | flops 62917632 | bytes 98821 | tf_op jit(solution)/shard_map/while/body/eval_jaxpr/dot_general | solution.py:86
  375.1 4.8 %fusion.173 = f32[3,512]{1,0:T(4,128)S(1)} fusion(f32[2560]{0:T(1024)S(1)} %get-tuple-element.504, f32[512]{0:T(512)S(1)} %bitcast.203, f32[2560]{0:T(1024)S(1)} %get-tuple-element.506, f32[512]{0:T(512)S(1)} %bitcast.204, f32[2560]{0:T(1024)S(1)} %get-tuple-element.508, f32[512]{0:T(512)S(1)} %bitcast.202, ...), kind=kOutput, calls=%fused_computation.119.clone.1 | convolution fusion | flops 62917632 | bytes 98821 | tf_op jit(solution)/shard_map/while/body/eval_jaxpr/dot_general | solution.py:86
  381.3 4.8 %fusion.173 = f32[3,512]{1,0:T(4,128)S(1)} fusion(f32[2560]{0:T(1024)S(1)} %get-tuple-element.504, f32[512]{0:T(512)S(1)} %bitcast.203, f32[2560]{0:T(1024)S(1)} %get-tuple-element.506, f32[512]{0:T(512)S(1)} %bitcast.204, f32[2560]{0:T(1024)S(1)} %get-tuple-element.508, f32[512]{0:T(512)S(1)} %bitcast.202, ...), kind=kOutput, calls=%fused_computation.119.clone.1 | convolution fusion | flops 62917632 | bytes 98821 | tf_op jit(solution)/shard_map/while/body/eval_jaxpr/dot_general | solution.py:86
  387.5 4.8 %fusion.173 = f32[3,512]{1,0:T(4,128)S(1)} fusion(f32[2560]{0:T(1024)S(1)} %get-tuple-element.504, f32[512]{0:T(512)S(1)} %bitcast.203, f32[2560]{0:T(1024)S(1)} %get-tuple-element.506, f32[512]{0:T(512)S(1)} %bitcast.204, f32[2560]{0:T(1024)S(1)} %get-tuple-element.508, f32[512]{0:T(512)S(1)} %bitcast.202, ...), kind=kOutput, calls=%fused_computation.119.clone.1 | convolution fusion | flops 62917632 | bytes 98821 | tf_op jit(solution)/shard_map/while/body/eval_jaxpr/dot_general | solution.py:86
  (154 shorter events, 40.3 us)
Async XLA Ops:
  48.5 13.5 %collective-permute-start = (f32[6,2560]{1,0:T(8,128)S(1)}, f32[6,2560]{1,0:T(8,128)S(1)}, u32[]{:S(2)}, u32[]{:S(2)}) collective-permute-start(f32[6,2560]{1,0:T(8,128)S(1)} %all_gather.12), channel_id=1, source_target_pairs={{0,8},{4,12},{8,16},{12,20},{16,24},{20,28},{1,9},{5,13},{9,17},{1... | collective-permute-start | bytes 184328 | tf_op jit(solution)/shard_map/ppermute | solution.py:17
  52.0 10.1 %collective-permute-start.1 = (f32[6,2560]{1,0:T(8,128)S(1)}, f32[6,2560]{1,0:T(8,128)S(1)}, u32[]{:S(2)}, u32[]{:S(2)}) collective-permute-start(f32[6,2560]{1,0:T(8,128)S(1)} %all_gather.12), channel_id=1, source_target_pairs={{0,4},{4,8},{8,12},{12,16},{16,20},{20,24},{24,28},{1,5},{5,9},{9,... | collective-permute-start | bytes 184328 | tf_op jit(solution)/shard_map/ppermute | solution.py:17
  56.2 7.4 %collective-permute-start.2 = (f32[6,2560]{1,0:T(8,128)S(1)}, f32[6,2560]{1,0:T(8,128)S(1)}, u32[]{:S(2)}, u32[]{:S(2)}) collective-permute-start(f32[6,2560]{1,0:T(8,128)S(1)} %all_gather.12), channel_id=1, source_target_pairs={{4,0},{8,4},{12,8},{16,12},{20,16},{24,20},{28,24},{5,1},{9,5},{13... | collective-permute-start | bytes 184328 | tf_op jit(solution)/shard_map/ppermute | solution.py:17
  58.1 6.3 %collective-permute-start.3 = (f32[6,2560]{1,0:T(8,128)S(1)}, f32[6,2560]{1,0:T(8,128)S(1)}, u32[]{:S(2)}, u32[]{:S(2)}) collective-permute-start(f32[6,2560]{1,0:T(8,128)S(1)} %all_gather.12), channel_id=1, source_target_pairs={{8,0},{12,4},{16,8},{20,12},{24,16},{28,20},{9,1},{13,5},{17,9},{2... | collective-permute-start | bytes 184328 | tf_op jit(solution)/shard_map/ppermute | solution.py:17
  62.1 2.4 copy-start
  64.5 71.7 %copy-start.1 = (f32[3,640]{1,0:T(4,128)S(1)}, f32[3,640]{1,0:T(4,128)}, u32[]{:S(2)}) copy-start(f32[3,640]{1,0:T(4,128)} %param.13) | copy-start | bytes 23044
  141.6 9.5 %collective-permute-start.4 = (f32[6,2560]{1,0:T(8,128)S(1)}, f32[6,2560]{1,0:T(8,128)S(1)}, u32[]{:S(2)}, u32[]{:S(2)}) collective-permute-start(f32[6,2560]{1,0:T(8,128)S(1)} %all_gather.13), channel_id=1, source_target_pairs={{0,8},{4,12},{8,16},{12,20},{16,24},{20,28},{1,9},{5,13},{9,17},{1... | collective-permute-start | bytes 184328 | tf_op jit(solution)/shard_map/ppermute | solution.py:17
  143.5 7.6 %collective-permute-start.5 = (f32[6,2560]{1,0:T(8,128)S(1)}, f32[6,2560]{1,0:T(8,128)S(1)}, u32[]{:S(2)}, u32[]{:S(2)}) collective-permute-start(f32[6,2560]{1,0:T(8,128)S(1)} %all_gather.13), channel_id=1, source_target_pairs={{0,4},{4,8},{8,12},{12,16},{16,20},{20,24},{24,28},{1,5},{5,9},{9,... | collective-permute-start | bytes 184328 | tf_op jit(solution)/shard_map/ppermute | solution.py:17
  146.4 7.4 %collective-permute-start.6 = (f32[6,2560]{1,0:T(8,128)S(1)}, f32[6,2560]{1,0:T(8,128)S(1)}, u32[]{:S(2)}, u32[]{:S(2)}) collective-permute-start(f32[6,2560]{1,0:T(8,128)S(1)} %all_gather.13), channel_id=1, source_target_pairs={{4,0},{8,4},{12,8},{16,12},{20,16},{24,20},{28,24},{5,1},{9,5},{13... | collective-permute-start | bytes 184328 | tf_op jit(solution)/shard_map/ppermute | solution.py:17
  149.4 6.3 %collective-permute-start.7 = (f32[6,2560]{1,0:T(8,128)S(1)}, f32[6,2560]{1,0:T(8,128)S(1)}, u32[]{:S(2)}, u32[]{:S(2)}) collective-permute-start(f32[6,2560]{1,0:T(8,128)S(1)} %all_gather.13), channel_id=1, source_target_pairs={{8,0},{12,4},{16,8},{20,12},{24,16},{28,20},{9,1},{13,5},{17,9},{2... | collective-permute-start | bytes 184328 | tf_op jit(solution)/shard_map/ppermute | solution.py:17
  232.0 9.8 %collective-permute-start.8 = (f32[6,2560]{1,0:T(8,128)S(1)}, f32[6,2560]{1,0:T(8,128)S(1)}, u32[]{:S(2)}, u32[]{:S(2)}) collective-permute-start(f32[6,2560]{1,0:T(8,128)S(1)} %all_gather.14), channel_id=1, source_target_pairs={{0,8},{4,12},{8,16},{12,20},{16,24},{20,28},{1,9},{5,13},{9,17},{1... | collective-permute-start | bytes 184328 | tf_op jit(solution)/shard_map/ppermute | solution.py:17
  234.1 7.7 %collective-permute-start.9 = (f32[6,2560]{1,0:T(8,128)S(1)}, f32[6,2560]{1,0:T(8,128)S(1)}, u32[]{:S(2)}, u32[]{:S(2)}) collective-permute-start(f32[6,2560]{1,0:T(8,128)S(1)} %all_gather.14), channel_id=1, source_target_pairs={{0,4},{4,8},{8,12},{12,16},{16,20},{20,24},{24,28},{1,5},{5,9},{9,... | collective-permute-start | bytes 184328 | tf_op jit(solution)/shard_map/ppermute | solution.py:17
  237.7 7.4 %collective-permute-start.10 = (f32[6,2560]{1,0:T(8,128)S(1)}, f32[6,2560]{1,0:T(8,128)S(1)}, u32[]{:S(2)}, u32[]{:S(2)}) collective-permute-start(f32[6,2560]{1,0:T(8,128)S(1)} %all_gather.14), channel_id=1, source_target_pairs={{4,0},{8,4},{12,8},{16,12},{20,16},{24,20},{28,24},{5,1},{9,5},{13... | collective-permute-start | bytes 184328 | tf_op jit(solution)/shard_map/ppermute | solution.py:17
  240.0 6.3 %collective-permute-start.11 = (f32[6,2560]{1,0:T(8,128)S(1)}, f32[6,2560]{1,0:T(8,128)S(1)}, u32[]{:S(2)}, u32[]{:S(2)}) collective-permute-start(f32[6,2560]{1,0:T(8,128)S(1)} %all_gather.14), channel_id=1, source_target_pairs={{8,0},{12,4},{16,8},{20,12},{24,16},{28,20},{9,1},{13,5},{17,9},{2... | collective-permute-start | bytes 184328 | tf_op jit(solution)/shard_map/ppermute | solution.py:17
  318.8 29.5 %copy-start.4 = (f32[3,640]{1,0:T(4,128)}, f32[3,640]{1,0:T(4,128)S(1)}, u32[]{:S(2)}) copy-start(f32[3,640]{1,0:T(4,128)S(1)} %multiply_add_fusion) | copy-start | bytes 23044
  324.1 13.4 %collective-permute-start.12 = (f32[6,2560]{1,0:T(8,128)S(1)}, f32[6,2560]{1,0:T(8,128)S(1)}, u32[]{:S(2)}, u32[]{:S(2)}) collective-permute-start(f32[6,2560]{1,0:T(8,128)S(1)} %all_gather.15), channel_id=1, source_target_pairs={{0,12},{4,16},{8,20},{12,24},{16,28},{1,13},{5,17},{9,21},{13,25},... | collective-permute-start | bytes 184328 | tf_op jit(solution)/shard_map/ppermute | solution.py:17
  326.3 12.8 %collective-permute-start.13 = (f32[6,2560]{1,0:T(8,128)S(1)}, f32[6,2560]{1,0:T(8,128)S(1)}, u32[]{:S(2)}, u32[]{:S(2)}) collective-permute-start(f32[6,2560]{1,0:T(8,128)S(1)} %all_gather.15), channel_id=1, source_target_pairs={{0,8},{4,12},{8,16},{12,20},{16,24},{20,28},{1,9},{5,13},{9,17},{1... | collective-permute-start | bytes 184328 | tf_op jit(solution)/shard_map/ppermute | solution.py:17
  330.3 8.9 %collective-permute-start.14 = (f32[6,2560]{1,0:T(8,128)S(1)}, f32[6,2560]{1,0:T(8,128)S(1)}, u32[]{:S(2)}, u32[]{:S(2)}) collective-permute-start(f32[6,2560]{1,0:T(8,128)S(1)} %all_gather.15), channel_id=1, source_target_pairs={{0,4},{4,8},{8,12},{12,16},{16,20},{20,24},{24,28},{1,5},{5,9},{9,... | collective-permute-start | bytes 184328 | tf_op jit(solution)/shard_map/ppermute | solution.py:17
  334.1 7.6 %collective-permute-start.15 = (f32[6,2560]{1,0:T(8,128)S(1)}, f32[6,2560]{1,0:T(8,128)S(1)}, u32[]{:S(2)}, u32[]{:S(2)}) collective-permute-start(f32[6,2560]{1,0:T(8,128)S(1)} %all_gather.15), channel_id=1, source_target_pairs={{4,0},{8,4},{12,8},{16,12},{20,16},{24,20},{28,24},{5,1},{9,5},{13... | collective-permute-start | bytes 184328 | tf_op jit(solution)/shard_map/ppermute | solution.py:17
  336.1 6.8 %collective-permute-start.16 = (f32[6,2560]{1,0:T(8,128)S(1)}, f32[6,2560]{1,0:T(8,128)S(1)}, u32[]{:S(2)}, u32[]{:S(2)}) collective-permute-start(f32[6,2560]{1,0:T(8,128)S(1)} %all_gather.15), channel_id=1, source_target_pairs={{8,0},{12,4},{16,8},{20,12},{24,16},{28,20},{9,1},{13,5},{17,9},{2... | collective-permute-start | bytes 184328 | tf_op jit(solution)/shard_map/ppermute | solution.py:17
  337.5 54.8 %copy-start.5 = (f32[3,4]{1,0:T(4,128)}, f32[3,4]{1,0:T(4,128)S(1)}, u32[]{:S(2)}) copy-start(f32[3,4]{1,0:T(4,128)S(1)} %multiply_add_fusion.7) | copy-start | bytes 148
  337.5 10.7 %collective-permute-start.17 = (f32[6,2560]{1,0:T(8,128)S(1)}, f32[6,2560]{1,0:T(8,128)S(1)}, u32[]{:S(2)}, u32[]{:S(2)}) collective-permute-start(f32[6,2560]{1,0:T(8,128)S(1)} %all_gather.15), channel_id=1, source_target_pairs={{12,0},{16,4},{20,8},{24,12},{28,16},{13,1},{17,5},{21,9},{25,13},... | collective-permute-start | bytes 184328 | tf_op jit(solution)/shard_map/ppermute | solution.py:17
  348.2 0.7 copy-start.2
  348.3 0.7 copy-start.3
where the time goes:
time: 395 us; the launch traced here: 393 us
  blocking collectives  185 us (47%)
  matrix products  124 us (31%)
  starting transfers between devices  44.3 us (11%)
  waiting for transfers between devices  20.4 us (5%)
  other arithmetic  9.73 us (2%)
  local copies, waits for them, and re-layouts  7.71 us (2%)
    psum x3, blocking collectives, shards(): lax.psum((local_dots, jnp.sum(image_head * image_head, axis=1), jnp.dot(i...  124 us
    dot_general x22, matrix products, add_slab(): jnp.dot(values, tile, precision=precise, preferred_element_type=jnp.float32)  121 us
    ppermute x18, starting transfers between devices, from_behind(): lax.ppermute(value, axis, [(source, source + steps) for source in range(i...  44.3 us
    psum x1, blocking collectives, shards(): lax.psum((jnp.sum(source_values * source_values, axis=1), jnp.dot(source_...  40.3 us
    all_gather x4, blocking collectives, near_slabs(): slab = lax.all_gather(block, 'grp', axis=1, tiled=True)  21.1 us
    ppermute x18, waiting for transfers between devices, from_behind(): lax.ppermute(value, axis, [(source, source + steps) for source in range(i...  20.4 us
  transfers between devices with their start and end apart: 18, of which 9 were waited for; matrix products, arithmetic and copies ran while one was open for 1% of the time, Pallas kernels for 0%

commit v1 on v0

--- a/solution.py
+++ b/solution.py
@@ -64,7 +64,12 @@
 
 
 def near_slabs(block, reach):
-    slab = lax.all_gather(block, "grp", axis=1, tiled=True)
+    ring = [block]
+    for hop in range(3):
+        ring.append(lax.ppermute(ring[-1], "grp", [(dev, (dev + 1) % 4) for dev in range(4)]))
+    slab = jnp.roll(
+        jnp.concatenate(ring[::-1], axis=1), (lax.axis_index("grp") + 1) * ring[0].shape[1], axis=1
+    )
     pieces = []
     for offset in range(-reach, reach + 1):
         if offset == 0:

time: 395 us -> 415 us (1.051)
  waiting for transfers between devices: 20.4 us -> 59.3 us
  blocking collectives: 185 us -> 164 us
    ppermute x0 -> x12, waiting for transfers between devices: none -> 37.3 us  [near_slabs(): lax.ppermute(ring[-1], 'grp', [(dev, (dev + 1) % 4) for dev in range(4)])]
    all_gather x4 -> x0, blocking collectives: 21.1 us -> none  [near_slabs(): slab = lax.all_gather(block, 'grp', axis=1, tiled=True)]
  transfers between devices with their start and end apart: 18 -> 30, of which waited for: 9 -> 21; matrix products, arithmetic and copies ran while one was open for 1% -> 1% of each run, Pallas kernels for 0% -> 0%
where the time goes in v1:
time: 415 us; the launch traced here: 413 us
  blocking collectives  164 us (40%)
  matrix products  124 us (30%)
  waiting for transfers between devices  59.3 us (14%)
  starting transfers between devices  44.8 us (11%)
  other arithmetic  11.3 us (3%)
  local copies, waits for them, and re-layouts  8.24 us (2%)
    psum x3, blocking collectives, shards(): lax.psum((local_dots, jnp.sum(image_head * image_head, axis=1), jnp.dot(i...  123 us
    dot_general x22, matrix products, add_slab(): jnp.dot(values, tile, precision=precise, preferred_element_type=jnp.float32)  121 us
    ppermute x18, starting transfers between devices, from_behind(): lax.ppermute(value, axis, [(source, source + steps) for source in range(i...  44.6 us
    psum x1, blocking collectives, shards(): lax.psum((jnp.sum(source_values * source_values, axis=1), jnp.dot(source_...  40.3 us
    ppermute x12, waiting for transfers between devices, near_slabs(): lax.ppermute(ring[-1], 'grp', [(dev, (dev + 1) % 4) for dev in range(4)])  37.3 us
    ppermute x18, waiting for transfers between devices, from_behind(): lax.ppermute(value, axis, [(source, source + steps) for source in range(i...  21.9 us
  transfers between devices with their start and end apart: 30, of which 21 were waited for; matrix products, arithmetic and copies ran while one was open for 1% of the time, Pallas kernels for 0%

profile of v1, /device:TPU:6, one launch (start us, length us, event | category | flops | bytes accessed | tf_op | source)
XLA Modules:
  0.0 413.2 jit_solution(10225324796095334106)
XLA Ops:
  1.5 40.3 %psum.70 = f32[3]{0:T(128)S(1)} all-reduce(f32[3]{0:T(128)S(1)} %multiply_reduce_fusion.9), channel_id=1, replica_groups=mesh['blk'=8,'grp'=4] {'blk','grp'}, use_global_device_ids=true, to_apply=%region_1.0 | all-reduce | flops 3 | bytes 24 | tf_op jit(solution)/shard_map/psum | solution.py:109
  43.3 3.2 collective-permute-done
  46.5 3.2 collective-permute-done.1
  54.0 3.4 collective-permute-start.3
  58.4 4.2 %collective-permute-start.4 = (f32[6,2560]{1,0:T(8,128)S(1)}, f32[6,2560]{1,0:T(8,128)S(1)}, u32[]{:S(2)}, u32[]{:S(2)}) collective-permute-start(f32[6,2560]{1,0:T(8,128)S(1)} %fusion.146), channel_id=1, source_target_pairs={{0,4},{4,8},{8,12},{12,16},{16,20},{20,24},{24,28},{1,5},{5,9},{9,... | collective-permute-start | bytes 184328 | tf_op jit(solution)/shard_map/ppermute | solution.py:17
  65.9 3.9 collective-permute-done.5
  71.0 29.7 %while.44 = (s32[]{:T(128)}, f32[3,640]{1,0:T(4,128)S(1)}, f32[5,3,2560]{2,1,0:T(4,128)S(1)}, f32[3,640]{1,0:T(4,128)S(1)}, f32[5,3,2560]{2,1,0:T(4,128)S(1)}, /*index=5*/s32[]{:T(128)}, s32[]{:T(128)}, s32[]{}, s32[]{}) while((s32[]{:T(128)}, f32[3,640]{1,0:T(4,128)S(1)}, f32[5,3,2560]{2,1,0:T(4,128)S(1)}, ...), condition=%wide.region_3.5_spmd.clone, body=%wide.region_2.4_spmd.clone.sunk | while | flops 77008640 | bytes 184975 | solution.py:96
  71.1 5.8 %fusion.199 = f32[3,640]{1,0:T(4,128)S(1)} fusion(f32[2560]{0:T(1024)S(1)} %get-tuple-element.470, f32[640]{0:T(1024)S(1)} %get-tuple-element.471, f32[2560]{0:T(1024)S(1)} %get-tuple-element.472, f32[640]{0:T(1024)S(1)} %get-tuple-element.473, f32[2560]{0:T(1024)S(1)} %get-tuple-element.474, f32[640]{0:T(1024)S(1)} %get-tuple-element.475, ...), kind=kOutput, calls=%fused_computation.20.clone.1 | convolution fusion | flops 77008640 | bytes 108037 | tf_op jit(solution)/shard_map/while/body/eval_jaxpr/dot_general | solution.py:91
  77.0 5.8 %fusion.199 = f32[3,640]{1,0:T(4,128)S(1)} fusion(f32[2560]{0:T(1024)S(1)} %get-tuple-element.470, f32[640]{0:T(1024)S(1)} %get-tuple-element.471, f32[2560]{0:T(1024)S(1)} %get-tuple-element.472, f32[640]{0:T(1024)S(1)} %get-tuple-element.473, f32[2560]{0:T(1024)S(1)} %get-tuple-element.474, f32[640]{0:T(1024)S(1)} %get-tuple-element.475, ...), kind=kOutput, calls=%fused_computation.20.clone.1 | convolution fusion | flops 77008640 | bytes 108037 | tf_op jit(solution)/shard_map/while/body/eval_jaxpr/dot_general | solution.py:91
  83.0 5.8 %fusion.199 = f32[3,640]{1,0:T(4,128)S(1)} fusion(f32[2560]{0:T(1024)S(1)} %get-tuple-element.470, f32[640]{0:T(1024)S(1)} %get-tuple-element.471, f32[2560]{0:T(1024)S(1)} %get-tuple-element.472, f32[640]{0:T(1024)S(1)} %get-tuple-element.473, f32[2560]{0:T(1024)S(1)} %get-tuple-element.474, f32[640]{0:T(1024)S(1)} %get-tuple-element.475, ...), kind=kOutput, calls=%fused_computation.20.clone.1 | convolution fusion | flops 77008640 | bytes 108037 | tf_op jit(solution)/shard_map/while/body/eval_jaxpr/dot_general | solution.py:91
  88.9 5.8 %fusion.199 = f32[3,640]{1,0:T(4,128)S(1)} fusion(f32[2560]{0:T(1024)S(1)} %get-tuple-element.470, f32[640]{0:T(1024)S(1)} %get-tuple-element.471, f32[2560]{0:T(1024)S(1)} %get-tuple-element.472, f32[640]{0:T(1024)S(1)} %get-tuple-element.473, f32[2560]{0:T(1024)S(1)} %get-tuple-element.474, f32[640]{0:T(1024)S(1)} %get-tuple-element.475, ...), kind=kOutput, calls=%fused_computation.20.clone.1 | convolution fusion | flops 77008640 | bytes 108037 | tf_op jit(solution)/shard_map/while/body/eval_jaxpr/dot_general | solution.py:91
  94.8 5.8 %fusion.199 = f32[3,640]{1,0:T(4,128)S(1)} fusion(f32[2560]{0:T(1024)S(1)} %get-tuple-element.470, f32[640]{0:T(1024)S(1)} %get-tuple-element.471, f32[2560]{0:T(1024)S(1)} %get-tuple-element.472, f32[640]{0:T(1024)S(1)} %get-tuple-element.473, f32[2560]{0:T(1024)S(1)} %get-tuple-element.474, f32[640]{0:T(1024)S(1)} %get-tuple-element.475, ...), kind=kOutput, calls=%fused_computation.20.clone.1 | convolution fusion | flops 77008640 | bytes 108037 | tf_op jit(solution)/shard_map/while/body/eval_jaxpr/dot_general | solution.py:91
  101.0 41.4 %all-reduce.2 = (f32[3]{0:T(128)S(1)}, f32[3,4]{1,0:T(4,128)S(1)}, f32[3,1]{0,1:T(1,128)S(1)}) all-reduce(f32[3]{0:T(128)S(1)} %get-tuple-element.233, f32[3,4]{1,0:T(4,128)S(1)} %convolution_bitcast_fusion, f32[3,1]{0,1:T(1,128)S(1)} %bitcast.208), channel_id=1, replica_groups=mesh['blk'=8,'grp'=4] {'blk','grp'}, use_global_device_ids=true, to_apply=%region_9.11 | all-reduce | flops 18 | bytes 144 | tf_op jit(solution)/shard_map/psum | solution.py:135
  142.8 3.2 collective-permute-done.7
  146.0 3.2 collective-permute-done.8
  149.2 3.2 collective-permute-done.9
  157.5 3.3 collective-permute-start.12
  167.2 29.7 %while.45 = (s32[]{:T(128)}, f32[3,640]{1,0:T(4,128)S(1)}, f32[5,3,2560]{2,1,0:T(4,128)S(1)}, f32[3,640]{1,0:T(4,128)S(1)}, f32[5,3,2560]{2,1,0:T(4,128)S(1)}, /*index=5*/s32[]{:T(128)}, s32[]{:T(128)}, s32[]{}, s32[]{}) while((s32[]{:T(128)}, f32[3,640]{1,0:T(4,128)S(1)}, f32[5,3,2560]{2,1,0:T(4,128)S(1)}, ...), condition=%wide.region_12.14_spmd.clone, body=%wide.region_11.13_spmd.clone.sunk | while | flops 77008640 | bytes 184975 | solution.py:96
  167.4 5.8 %fusion.202 = f32[3,640]{1,0:T(4,128)S(1)} fusion(f32[2560]{0:T(1024)S(1)} %get-tuple-element.481, f32[640]{0:T(1024)S(1)} %get-tuple-element.482, f32[2560]{0:T(1024)S(1)} %get-tuple-element.483, f32[640]{0:T(1024)S(1)} %get-tuple-element.484, f32[2560]{0:T(1024)S(1)} %get-tuple-element.485, f32[640]{0:T(1024)S(1)} %get-tuple-element.486, ...), kind=kOutput, calls=%fused_computation.52.clone.1 | convolution fusion | flops 77008640 | bytes 108037 | tf_op jit(solution)/shard_map/while/body/eval_jaxpr/dot_general | solution.py:91
  173.3 5.8 %fusion.202 = f32[3,640]{1,0:T(4,128)S(1)} fusion(f32[2560]{0:T(1024)S(1)} %get-tuple-element.481, f32[640]{0:T(1024)S(1)} %get-tuple-element.482, f32[2560]{0:T(1024)S(1)} %get-tuple-element.483, f32[640]{0:T(1024)S(1)} %get-tuple-element.484, f32[2560]{0:T(1024)S(1)} %get-tuple-element.485, f32[640]{0:T(1024)S(1)} %get-tuple-element.486, ...), kind=kOutput, calls=%fused_computation.52.clone.1 | convolution fusion | flops 77008640 | bytes 108037 | tf_op jit(solution)/shard_map/while/body/eval_jaxpr/dot_general | solution.py:91
  179.2 5.8 %fusion.202 = f32[3,640]{1,0:T(4,128)S(1)} fusion(f32[2560]{0:T(1024)S(1)} %get-tuple-element.481, f32[640]{0:T(1024)S(1)} %get-tuple-element.482, f32[2560]{0:T(1024)S(1)} %get-tuple-element.483, f32[640]{0:T(1024)S(1)} %get-tuple-element.484, f32[2560]{0:T(1024)S(1)} %get-tuple-element.485, f32[640]{0:T(1024)S(1)} %get-tuple-element.486, ...), kind=kOutput, calls=%fused_computation.52.clone.1 | convolution fusion | flops 77008640 | bytes 108037 | tf_op jit(solution)/shard_map/while/body/eval_jaxpr/dot_general | solution.py:91
  185.2 5.8 %fusion.202 = f32[3,640]{1,0:T(4,128)S(1)} fusion(f32[2560]{0:T(1024)S(1)} %get-tuple-element.481, f32[640]{0:T(1024)S(1)} %get-tuple-element.482, f32[2560]{0:T(1024)S(1)} %get-tuple-element.483, f32[640]{0:T(1024)S(1)} %get-tuple-element.484, f32[2560]{0:T(1024)S(1)} %get-tuple-element.485, f32[640]{0:T(1024)S(1)} %get-tuple-element.486, ...), kind=kOutput, calls=%fused_computation.52.clone.1 | convolution fusion | flops 77008640 | bytes 108037 | tf_op jit(solution)/shard_map/while/body/eval_jaxpr/dot_general | solution.py:91
  191.1 5.8 %fusion.202 = f32[3,640]{1,0:T(4,128)S(1)} fusion(f32[2560]{0:T(1024)S(1)} %get-tuple-element.481, f32[640]{0:T(1024)S(1)} %get-tuple-element.482, f32[2560]{0:T(1024)S(1)} %get-tuple-element.483, f32[640]{0:T(1024)S(1)} %get-tuple-element.484, f32[2560]{0:T(1024)S(1)} %get-tuple-element.485, f32[640]{0:T(1024)S(1)} %get-tuple-element.486, ...), kind=kOutput, calls=%fused_computation.52.clone.1 | convolution fusion | flops 77008640 | bytes 108037 | tf_op jit(solution)/shard_map/while/body/eval_jaxpr/dot_general | solution.py:91
  197.3 40.3 %all-reduce.1 = (f32[3]{0:T(128)S(1)}, f32[3,4]{1,0:T(4,128)S(1)}, f32[3,2]{0,1:T(2,128)S(1)}) all-reduce(f32[3]{0:T(128)S(1)} %get-tuple-element.230, f32[3,4]{1,0:T(4,128)S(1)} %fusion.171, f32[3,2]{0,1:T(2,128)S(1)} %pad_maximum_fusion.5), channel_id=1, replica_groups=mesh['blk'=8,'grp'=4] {'blk','grp'}, use_global_device_ids=true, to_apply=%region_20.22 | all-reduce | flops 21 | bytes 168 | tf_op jit(solution)/shard_map/psum | solution.py:135
  238.1 3.2 collective-permute-done.14
  241.3 3.2 collective-permute-done.15
  250.3 3.4 collective-permute-start.18
  257.7 3.2 collective-permute-done.19
  262.6 29.7 %while.46 = (s32[]{:T(128)}, f32[3,640]{1,0:T(4,128)S(1)}, f32[5,3,2560]{2,1,0:T(4,128)S(1)}, f32[3,640]{1,0:T(4,128)S(1)}, f32[5,3,2560]{2,1,0:T(4,128)S(1)}, /*index=5*/s32[]{:T(128)}, s32[]{:T(128)}, s32[]{}, s32[]{}) while((s32[]{:T(128)}, f32[3,640]{1,0:T(4,128)S(1)}, f32[5,3,2560]{2,1,0:T(4,128)S(1)}, ...), condition=%wide.region_23.25_spmd.clone, body=%wide.region_22.24_spmd.clone.sunk | while | flops 77008640 | bytes 184975 | solution.py:96
  262.7 5.8 %fusion.205 = f32[3,640]{1,0:T(4,128)S(1)} fusion(f32[2560]{0:T(1024)S(1)} %get-tuple-element.492, f32[640]{0:T(1024)S(1)} %get-tuple-element.493, f32[2560]{0:T(1024)S(1)} %get-tuple-element.494, f32[640]{0:T(1024)S(1)} %get-tuple-element.495, f32[2560]{0:T(1024)S(1)} %get-tuple-element.496, f32[640]{0:T(1024)S(1)} %get-tuple-element.497, ...), kind=kOutput, calls=%fused_computation.84.clone.1 | convolution fusion | flops 77008640 | bytes 108037 | tf_op jit(solution)/shard_map/while/body/eval_jaxpr/dot_general | solution.py:91
  268.6 5.8 %fusion.205 = f32[3,640]{1,0:T(4,128)S(1)} fusion(f32[2560]{0:T(1024)S(1)} %get-tuple-element.492, f32[640]{0:T(1024)S(1)} %get-tuple-element.493, f32[2560]{0:T(1024)S(1)} %get-tuple-element.494, f32[640]{0:T(1024)S(1)} %get-tuple-element.495, f32[2560]{0:T(1024)S(1)} %get-tuple-element.496, f32[640]{0:T(1024)S(1)} %get-tuple-element.497, ...), kind=kOutput, calls=%fused_computation.84.clone.1 | convolution fusion | flops 77008640 | bytes 108037 | tf_op jit(solution)/shard_map/while/body/eval_jaxpr/dot_general | solution.py:91
  274.6 5.8 %fusion.205 = f32[3,640]{1,0:T(4,128)S(1)} fusion(f32[2560]{0:T(1024)S(1)} %get-tuple-element.492, f32[640]{0:T(1024)S(1)} %get-tuple-element.493, f32[2560]{0:T(1024)S(1)} %get-tuple-element.494, f32[640]{0:T(1024)S(1)} %get-tuple-element.495, f32[2560]{0:T(1024)S(1)} %get-tuple-element.496, f32[640]{0:T(1024)S(1)} %get-tuple-element.497, ...), kind=kOutput, calls=%fused_computation.84.clone.1 | convolution fusion | flops 77008640 | bytes 108037 | tf_op jit(solution)/shard_map/while/body/eval_jaxpr/dot_general | solution.py:91
  280.5 5.8 %fusion.205 = f32[3,640]{1,0:T(4,128)S(1)} fusion(f32[2560]{0:T(1024)S(1)} %get-tuple-element.492, f32[640]{0:T(1024)S(1)} %get-tuple-element.493, f32[2560]{0:T(1024)S(1)} %get-tuple-element.494, f32[640]{0:T(1024)S(1)} %get-tuple-element.495, f32[2560]{0:T(1024)S(1)} %get-tuple-element.496, f32[640]{0:T(1024)S(1)} %get-tuple-element.497, ...), kind=kOutput, calls=%fused_computation.84.clone.1 | convolution fusion | flops 77008640 | bytes 108037 | tf_op jit(solution)/shard_map/while/body/eval_jaxpr/dot_general | solution.py:91
  286.5 5.8 %fusion.205 = f32[3,640]{1,0:T(4,128)S(1)} fusion(f32[2560]{0:T(1024)S(1)} %get-tuple-element.492, f32[640]{0:T(1024)S(1)} %get-tuple-element.493, f32[2560]{0:T(1024)S(1)} %get-tuple-element.494, f32[640]{0:T(1024)S(1)} %get-tuple-element.495, f32[2560]{0:T(1024)S(1)} %get-tuple-element.496, f32[640]{0:T(1024)S(1)} %get-tuple-element.497, ...), kind=kOutput, calls=%fused_computation.84.clone.1 | convolution fusion | flops 77008640 | bytes 108037 | tf_op jit(solution)/shard_map/while/body/eval_jaxpr/dot_general | solution.py:91
  292.7 41.7 %all-reduce = (f32[3]{0:T(128)S(1)}, f32[3,4]{1,0:T(4,128)S(1)}, f32[3,3]{0,1:T(4,128)S(1)}) all-reduce(f32[3]{0:T(128)S(1)} %get-tuple-element.226, f32[3,4]{1,0:T(4,128)S(1)} %fusion.170, f32[3,3]{0,1:T(4,128)S(1)} %pad_maximum_fusion.4), channel_id=1, replica_groups=mesh['blk'=8,'grp'=4] {'blk','grp'}, use_global_device_ids=true, to_apply=%region_33.35 | all-reduce | flops 24 | bytes 192 | tf_op jit(solution)/shard_map/psum | solution.py:135
  334.9 3.2 collective-permute-done.21
  341.3 3.2 collective-permute-done.23
  347.2 4.0 collective-permute-start.25
  351.2 3.7 collective-permute-start.26
  363.4 4.1 collective-permute-done.29
  368.2 44.2 %while.47 = (s32[]{:T(128)}, f32[3,512]{1,0:T(4,128)S(1)}, f32[7,3,2560]{2,1,0:T(4,128)S(1)}, s32[7]{0:T(128)S(1)}, s32[512]{0:T(512)S(1)}, /*index=5*/f32[3,512...) while((s32[]{:T(128)}, f32[3,512]{1,0:T(4,128)S(1)}, ...), condition=%wide.region_36.38_spmd.clone, body=%wide.region_35.37_spmd.clone.sunk | while | flops 62919172 | bytes 175279 | solution.py:96
  369.7 4.8 %fusion.209 = f32[3,512]{1,0:T(4,128)S(1)} fusion(f32[2560]{0:T(1024)S(1)} %get-tuple-element.505, f32[512]{0:T(512)S(1)} %bitcast.203, f32[2560]{0:T(1024)S(1)} %get-tuple-element.507, f32[512]{0:T(512)S(1)} %bitcast.204, f32[2560]{0:T(1024)S(1)} %get-tuple-element.509, f32[512]{0:T(512)S(1)} %bitcast.202, ...), kind=kOutput, calls=%fused_computation.119.clone.1 | convolution fusion | flops 62917632 | bytes 98821 | tf_op jit(solution)/shard_map/while/body/eval_jaxpr/dot_general | solution.py:91
  376.0 4.8 %fusion.209 = f32[3,512]{1,0:T(4,128)S(1)} fusion(f32[2560]{0:T(1024)S(1)} %get-tuple-element.505, f32[512]{0:T(512)S(1)} %bitcast.203, f32[2560]{0:T(1024)S(1)} %get-tuple-element.507, f32[512]{0:T(512)S(1)} %bitcast.204, f32[2560]{0:T(1024)S(1)} %get-tuple-element.509, f32[512]{0:T(512)S(1)} %bitcast.202, ...), kind=kOutput, calls=%fused_computation.119.clone.1 | convolution fusion | flops 62917632 | bytes 98821 | tf_op jit(solution)/shard_map/while/body/eval_jaxpr/dot_general | solution.py:91
  382.3 4.8 %fusion.209 = f32[3,512]{1,0:T(4,128)S(1)} fusion(f32[2560]{0:T(1024)S(1)} %get-tuple-element.505, f32[512]{0:T(512)S(1)} %bitcast.203, f32[2560]{0:T(1024)S(1)} %get-tuple-element.507, f32[512]{0:T(512)S(1)} %bitcast.204, f32[2560]{0:T(1024)S(1)} %get-tuple-element.509, f32[512]{0:T(512)S(1)} %bitcast.202, ...), kind=kOutput, calls=%fused_computation.119.clone.1 | convolution fusion | flops 62917632 | bytes 98821 | tf_op jit(solution)/shard_map/while/body/eval_jaxpr/dot_general | solution.py:91
  388.6 4.8 %fusion.209 = f32[3,512]{1,0:T(4,128)S(1)} fusion(f32[2560]{0:T(1024)S(1)} %get-tuple-element.505, f32[512]{0:T(512)S(1)} %bitcast.203, f32[2560]{0:T(1024)S(1)} %get-tuple-element.507, f32[512]{0:T(512)S(1)} %bitcast.204, f32[2560]{0:T(1024)S(1)} %get-tuple-element.509, f32[512]{0:T(512)S(1)} %bitcast.202, ...), kind=kOutput, calls=%fused_computation.119.clone.1 | convolution fusion | flops 62917632 | bytes 98821 | tf_op jit(solution)/shard_map/while/body/eval_jaxpr/dot_general | solution.py:91
  394.9 4.8 %fusion.209 = f32[3,512]{1,0:T(4,128)S(1)} fusion(f32[2560]{0:T(1024)S(1)} %get-tuple-element.505, f32[512]{0:T(512)S(1)} %bitcast.203, f32[2560]{0:T(1024)S(1)} %get-tuple-element.507, f32[512]{0:T(512)S(1)} %bitcast.204, f32[2560]{0:T(1024)S(1)} %get-tuple-element.509, f32[512]{0:T(512)S(1)} %bitcast.202, ...), kind=kOutput, calls=%fused_computation.119.clone.1 | convolution fusion | flops 62917632 | bytes 98821 | tf_op jit(solution)/shard_map/while/body/eval_jaxpr/dot_general | solution.py:91
  401.2 4.8 %fusion.209 = f32[3,512]{1,0:T(4,128)S(1)} fusion(f32[2560]{0:T(1024)S(1)} %get-tuple-element.505, f32[512]{0:T(512)S(1)} %bitcast.203, f32[2560]{0:T(1024)S(1)} %get-tuple-element.507, f32[512]{0:T(512)S(1)} %bitcast.204, f32[2560]{0:T(1024)S(1)} %get-tuple-element.509, f32[512]{0:T(512)S(1)} %bitcast.202, ...), kind=kOutput, calls=%fused_computation.119.clone.1 | convolution fusion | flops 62917632 | bytes 98821 | tf_op jit(solution)/shard_map/while/body/eval_jaxpr/dot_general | solution.py:91
  407.6 4.8 %fusion.209 = f32[3,512]{1,0:T(4,128)S(1)} fusion(f32[2560]{0:T(1024)S(1)} %get-tuple-element.505, f32[512]{0:T(512)S(1)} %bitcast.203, f32[2560]{0:T(1024)S(1)} %get-tuple-element.507, f32[512]{0:T(512)S(1)} %bitcast.204, f32[2560]{0:T(1024)S(1)} %get-tuple-element.509, f32[512]{0:T(512)S(1)} %bitcast.202, ...), kind=kOutput, calls=%fused_computation.119.clone.1 | convolution fusion | flops 62917632 | bytes 98821 | tf_op jit(solution)/shard_map/while/body/eval_jaxpr/dot_general | solution.py:91
  (178 shorter events, 64.7 us)
Async XLA Ops:
  43.3 3.3 collective-permute-start
  46.5 3.2 collective-permute-start.1
  49.8 3.2 collective-permute-start.2
  54.0 11.8 %collective-permute-start.3 = (f32[6,2560]{1,0:T(8,128)S(1)}, f32[6,2560]{1,0:T(8,128)S(1)}, u32[]{:S(2)}, u32[]{:S(2)}) collective-permute-start(f32[6,2560]{1,0:T(8,128)S(1)} %fusion.146), channel_id=1, source_target_pairs={{0,8},{4,12},{8,16},{12,20},{16,24},{20,28},{1,9},{5,13},{9,17},{1... | collective-permute-start | bytes 184328 | tf_op jit(solution)/shard_map/ppermute | solution.py:17
  58.4 7.5 %collective-permute-start.4 = (f32[6,2560]{1,0:T(8,128)S(1)}, f32[6,2560]{1,0:T(8,128)S(1)}, u32[]{:S(2)}, u32[]{:S(2)}) collective-permute-start(f32[6,2560]{1,0:T(8,128)S(1)} %fusion.146), channel_id=1, source_target_pairs={{0,4},{4,8},{8,12},{12,16},{16,20},{20,24},{24,28},{1,5},{5,9},{9,... | collective-permute-start | bytes 184328 | tf_op jit(solution)/shard_map/ppermute | solution.py:17
  62.6 7.2 %collective-permute-start.5 = (f32[6,2560]{1,0:T(8,128)S(1)}, f32[6,2560]{1,0:T(8,128)S(1)}, u32[]{:S(2)}, u32[]{:S(2)}) collective-permute-start(f32[6,2560]{1,0:T(8,128)S(1)} %fusion.146), channel_id=1, source_target_pairs={{4,0},{8,4},{12,8},{16,12},{20,16},{24,20},{28,24},{5,1},{9,5},{13... | collective-permute-start | bytes 184328 | tf_op jit(solution)/shard_map/ppermute | solution.py:17
  64.5 6.3 %collective-permute-start.6 = (f32[6,2560]{1,0:T(8,128)S(1)}, f32[6,2560]{1,0:T(8,128)S(1)}, u32[]{:S(2)}, u32[]{:S(2)}) collective-permute-start(f32[6,2560]{1,0:T(8,128)S(1)} %fusion.146), channel_id=1, source_target_pairs={{8,0},{12,4},{16,8},{20,12},{24,16},{28,20},{9,1},{13,5},{17,9},{2... | collective-permute-start | bytes 184328 | tf_op jit(solution)/shard_map/ppermute | solution.py:17
  65.9 5.1 %copy-start = (f32[3,640]{1,0:T(4,128)S(1)}, f32[3,640]{1,0:T(4,128)}, u32[]{:S(2)}) copy-start(f32[3,640]{1,0:T(4,128)} %param.14) | copy-start | bytes 23044
  70.9 71.7 %copy-start.1 = (f32[3,640]{1,0:T(4,128)S(1)}, f32[3,640]{1,0:T(4,128)}, u32[]{:S(2)}) copy-start(f32[3,640]{1,0:T(4,128)} %param.15) | copy-start | bytes 23044
  142.8 3.3 collective-permute-start.7
  146.0 3.2 collective-permute-start.8
  149.2 3.2 collective-permute-start.9
  152.8 9.5 %collective-permute-start.10 = (f32[6,2560]{1,0:T(8,128)S(1)}, f32[6,2560]{1,0:T(8,128)S(1)}, u32[]{:S(2)}, u32[]{:S(2)}) collective-permute-start(f32[6,2560]{1,0:T(8,128)S(1)} %fusion.137), channel_id=1, source_target_pairs={{0,8},{4,12},{8,16},{12,20},{16,24},{20,28},{1,9},{5,13},{9,17},{1... | collective-permute-start | bytes 184328 | tf_op jit(solution)/shard_map/ppermute | solution.py:17
  154.9 7.4 %collective-permute-start.11 = (f32[6,2560]{1,0:T(8,128)S(1)}, f32[6,2560]{1,0:T(8,128)S(1)}, u32[]{:S(2)}, u32[]{:S(2)}) collective-permute-start(f32[6,2560]{1,0:T(8,128)S(1)} %fusion.137), channel_id=1, source_target_pairs={{0,4},{4,8},{8,12},{12,16},{16,20},{20,24},{24,28},{1,5},{5,9},{9,... | collective-permute-start | bytes 184328 | tf_op jit(solution)/shard_map/ppermute | solution.py:17
  157.5 7.2 %collective-permute-start.12 = (f32[6,2560]{1,0:T(8,128)S(1)}, f32[6,2560]{1,0:T(8,128)S(1)}, u32[]{:S(2)}, u32[]{:S(2)}) collective-permute-start(f32[6,2560]{1,0:T(8,128)S(1)} %fusion.137), channel_id=1, source_target_pairs={{4,0},{8,4},{12,8},{16,12},{20,16},{24,20},{28,24},{5,1},{9,5},{13... | collective-permute-start | bytes 184328 | tf_op jit(solution)/shard_map/ppermute | solution.py:17
  160.8 6.3 %collective-permute-start.13 = (f32[6,2560]{1,0:T(8,128)S(1)}, f32[6,2560]{1,0:T(8,128)S(1)}, u32[]{:S(2)}, u32[]{:S(2)}) collective-permute-start(f32[6,2560]{1,0:T(8,128)S(1)} %fusion.137), channel_id=1, source_target_pairs={{8,0},{12,4},{16,8},{20,12},{24,16},{28,20},{9,1},{13,5},{17,9},{2... | collective-permute-start | bytes 184328 | tf_op jit(solution)/shard_map/ppermute | solution.py:17
  238.0 3.3 collective-permute-start.14
  241.3 3.2 collective-permute-start.15
  244.5 3.2 collective-permute-start.16
  248.0 9.6 %collective-permute-start.17 = (f32[6,2560]{1,0:T(8,128)S(1)}, f32[6,2560]{1,0:T(8,128)S(1)}, u32[]{:S(2)}, u32[]{:S(2)}) collective-permute-start(f32[6,2560]{1,0:T(8,128)S(1)} %fusion.128), channel_id=1, source_target_pairs={{0,8},{4,12},{8,16},{12,20},{16,24},{20,28},{1,9},{5,13},{9,17},{1... | collective-permute-start | bytes 184328 | tf_op jit(solution)/shard_map/ppermute | solution.py:17
  250.3 7.4 %collective-permute-start.18 = (f32[6,2560]{1,0:T(8,128)S(1)}, f32[6,2560]{1,0:T(8,128)S(1)}, u32[]{:S(2)}, u32[]{:S(2)}) collective-permute-start(f32[6,2560]{1,0:T(8,128)S(1)} %fusion.128), channel_id=1, source_target_pairs={{0,4},{4,8},{8,12},{12,16},{16,20},{20,24},{24,28},{1,5},{5,9},{9,... | collective-permute-start | bytes 184328 | tf_op jit(solution)/shard_map/ppermute | solution.py:17
  253.7 7.2 %collective-permute-start.19 = (f32[6,2560]{1,0:T(8,128)S(1)}, f32[6,2560]{1,0:T(8,128)S(1)}, u32[]{:S(2)}, u32[]{:S(2)}) collective-permute-start(f32[6,2560]{1,0:T(8,128)S(1)} %fusion.128), channel_id=1, source_target_pairs={{4,0},{8,4},{12,8},{16,12},{20,16},{24,20},{28,24},{5,1},{9,5},{13... | collective-permute-start | bytes 184328 | tf_op jit(solution)/shard_map/ppermute | solution.py:17
  256.1 6.3 %collective-permute-start.20 = (f32[6,2560]{1,0:T(8,128)S(1)}, f32[6,2560]{1,0:T(8,128)S(1)}, u32[]{:S(2)}, u32[]{:S(2)}) collective-permute-start(f32[6,2560]{1,0:T(8,128)S(1)} %fusion.128), channel_id=1, source_target_pairs={{8,0},{12,4},{16,8},{20,12},{24,16},{28,20},{9,1},{13,5},{17,9},{2... | collective-permute-start | bytes 184328 | tf_op jit(solution)/shard_map/ppermute | solution.py:17
  262.5 75.5 %copy-start.2 = (f32[3,512]{1,0:T(4,128)S(1)}, f32[3,512]{1,0:T(4,128)}, u32[]{:S(2)}) copy-start(f32[3,512]{1,0:T(4,128)} %param.16) | copy-start | bytes 18436
  334.8 28.6 %copy-start.3 = (f32[3,640]{1,0:T(4,128)}, f32[3,640]{1,0:T(4,128)S(1)}, u32[]{:S(2)}) copy-start(f32[3,640]{1,0:T(4,128)S(1)} %multiply_add_fusion) | copy-start | bytes 23044
  334.8 3.3 collective-permute-start.21
  338.1 3.2 collective-permute-start.22
  341.3 3.2 collective-permute-start.23
  344.8 13.5 %collective-permute-start.24 = (f32[6,2560]{1,0:T(8,128)S(1)}, f32[6,2560]{1,0:T(8,128)S(1)}, u32[]{:S(2)}, u32[]{:S(2)}) collective-permute-start(f32[6,2560]{1,0:T(8,128)S(1)} %fusion.119), channel_id=1, source_target_pairs={{0,12},{4,16},{8,20},{12,24},{16,28},{1,13},{5,17},{9,21},{13,25},... | collective-permute-start | bytes 184328 | tf_op jit(solution)/shard_map/ppermute | solution.py:17
  347.2 65.2 %copy-start.5 = (f32[3,4]{1,0:T(4,128)}, f32[3,4]{1,0:T(4,128)S(1)}, u32[]{:S(2)}) copy-start(f32[3,4]{1,0:T(4,128)S(1)} %multiply_add_fusion.7) | copy-start | bytes 148
  347.2 12.7 %collective-permute-start.25 = (f32[6,2560]{1,0:T(8,128)S(1)}, f32[6,2560]{1,0:T(8,128)S(1)}, u32[]{:S(2)}, u32[]{:S(2)}) collective-permute-start(f32[6,2560]{1,0:T(8,128)S(1)} %fusion.119), channel_id=1, source_target_pairs={{0,8},{4,12},{8,16},{12,20},{16,24},{20,28},{1,9},{5,13},{9,17},{1... | collective-permute-start | bytes 184328 | tf_op jit(solution)/shard_map/ppermute | solution.py:17
  351.2 8.8 %collective-permute-start.26 = (f32[6,2560]{1,0:T(8,128)S(1)}, f32[6,2560]{1,0:T(8,128)S(1)}, u32[]{:S(2)}, u32[]{:S(2)}) collective-permute-start(f32[6,2560]{1,0:T(8,128)S(1)} %fusion.119), channel_id=1, source_target_pairs={{0,4},{4,8},{8,12},{12,16},{16,20},{20,24},{24,28},{1,5},{5,9},{9,... | collective-permute-start | bytes 184328 | tf_op jit(solution)/shard_map/ppermute | solution.py:17
  354.9 7.2 %collective-permute-start.27 = (f32[6,2560]{1,0:T(8,128)S(1)}, f32[6,2560]{1,0:T(8,128)S(1)}, u32[]{:S(2)}, u32[]{:S(2)}) collective-permute-start(f32[6,2560]{1,0:T(8,128)S(1)} %fusion.119), channel_id=1, source_target_pairs={{4,0},{8,4},{12,8},{16,12},{20,16},{24,20},{28,24},{5,1},{9,5},{13... | collective-permute-start | bytes 184328 | tf_op jit(solution)/shard_map/ppermute | solution.py:17
  357.1 6.3 %collective-permute-start.28 = (f32[6,2560]{1,0:T(8,128)S(1)}, f32[6,2560]{1,0:T(8,128)S(1)}, u32[]{:S(2)}, u32[]{:S(2)}) collective-permute-start(f32[6,2560]{1,0:T(8,128)S(1)} %fusion.119), channel_id=1, source_target_pairs={{8,0},{12,4},{16,8},{20,12},{24,16},{28,20},{9,1},{13,5},{17,9},{2... | collective-permute-start | bytes 184328 | tf_op jit(solution)/shard_map/ppermute | solution.py:17
  358.4 9.1 %collective-permute-start.29 = (f32[6,2560]{1,0:T(8,128)S(1)}, f32[6,2560]{1,0:T(8,128)S(1)}, u32[]{:S(2)}, u32[]{:S(2)}) collective-permute-start(f32[6,2560]{1,0:T(8,128)S(1)} %fusion.119), channel_id=1, source_target_pairs={{12,0},{16,4},{20,8},{24,12},{28,16},{13,1},{17,5},{21,9},{25,13},... | collective-permute-start | bytes 184328 | tf_op jit(solution)/shard_map/ppermute | solution.py:17
  367.5 0.7 copy-start.4
